TPU v7x, 256 devices: a whole 4x4x8 slice. The times are simulated.
256 devices in a mesh: seq: 32 (over y, x, z_lo), head: 8 (over z_hi, core).
Axes of the slice: x: 4, y: 4, z: 8 (z_hi: 4, z_lo: 2; z = z_hi * 2 + z_lo), core: 2. Of those that a mesh axis runs over, the one named last changes fastest.
Arguments:
- queries: bfloat16 [8192, 4096], P(('seq', 'head')), may hold values from -10 to 10
- keys: bfloat16 [8192, 1024], P(('seq', 'head')), may hold values from -10 to 10
- block_pos: int32 [64], replicated, may hold values from 0 to 63, each once
- query_map: float32 [32, 128, 128], P('head'), may hold values from -4 to 4
- key_map: float32 [8, 128, 128], P('head'), may hold values from -4 to 4
Outputs:
- query_map_gradient: float32 [32, 128, 128], P('head')
- key_map_gradient: float32 [8, 128, 128], P('head')
Inputs may be any that keep to these rules, and one draw needn't show every extreme that they name: A permutation: stored block g (token rows g * 128 to (g + 1) * 128 - 1) holds position block block_pos[g]; position blocks below 32 form the first sequence, the others the second.
All inputs are finite; a program needn't handle non-finite values.
Results may differ from a plain program's by a relative error of at most 0.0021.
Values may be sent and summed in bfloat16 or wider, within the bound.
A program may use at most 64 MiB of HBM per device.

v0:
```python
import math

import jax
import jax.numpy as jnp
from jax import lax
from jax.sharding import PartitionSpec as P

HEAD_SIZE = 128
BLK = 128


HIGHEST = lax.Precision.HIGHEST
NEG_FLOOR = -1e30


def sent_together(arrays, axis, dim, along):
    widths = [a.shape[along] for a in arrays]
    both = jnp.concatenate(arrays, axis=along)
    whole = lax.all_gather(both, axis, axis=dim, tiled=True)
    return tuple(jnp.split(whole, [sum(widths[:k]) for k in range(1, len(widths))], axis=along))


def padded_to(lines, count):
    spare = -len(lines) % count
    return jnp.pad(lines, [(0, spare)] + [(0, 0)] * (lines.ndim - 1))


def in_order(parts, dim):
    parts = jnp.moveaxis(parts, 0, dim)
    shape = parts.shape
    return parts.reshape(*shape[:dim], shape[dim] * shape[dim + 1], *shape[dim + 2 :])


def copy_for_each(value, axis):
    copies = jnp.broadcast_to(value, (lax.axis_size(axis), *value.shape))
    return lax.all_to_all(copies, axis, split_axis=0, concat_axis=0, tiled=True)


def collect(value, axis, dim):
    return in_order(copy_for_each(value, axis), dim)


def split_up(value, dim, count):
    before, after = (value.shape[:dim], value.shape[dim + 1 :])
    return jnp.moveaxis(value.reshape(*before, count, -1, *after), dim, 0)


def summed_on_arrival(value, axis, dim):
    count = lax.axis_size(axis)
    parts = lax.all_to_all(split_up(value, dim, count), axis, 0, 0, tiled=True)
    return jnp.sum(parts, axis=0)


def sum_by_parts(value, axes):
    padded = padded_to(value, lax.axis_size(axes))
    whole = collect(summed_on_arrival(padded, axes, 0), axes, 0)
    return lax.slice_in_dim(whole, 0, len(value)).reshape(value.shape)


def together(arrays, axis):
    vector, at, outs = (jnp.concatenate([a.reshape(-1) for a in arrays]), 0, [])
    so_far = sum_by_parts(vector, axis)
    for a in arrays:
        outs.append(so_far[at : at + a.size].reshape(a.shape))
        at += a.size
    return tuple(outs)


def softmax_pair(logits):
    return jnp.concatenate(
        [jax.nn.softmax(logits, axis=-1), jax.nn.softmax(-logits, axis=-1)], axis=-1
    )


def feature_grad(feature, upstream):
    half_width = feature.shape[-1] // 2
    positive, negative = (feature[..., :half_width], feature[..., half_width:])
    grad_positive, grad_negative = (upstream[..., :half_width], upstream[..., half_width:])
    first = positive * (grad_positive - jnp.sum(grad_positive * positive, axis=-1, keepdims=True))
    second = negative * (grad_negative - jnp.sum(grad_negative * negative, axis=-1, keepdims=True))
    return first - second


def row_places(row_index, block_pos, seq_count):
    stored = row_index // BLK
    lookup = stored[:, None] == jnp.arange(block_pos.shape[0], dtype=jnp.int32)[None, :]
    blocks = jnp.sum(jnp.where(lookup, block_pos[None, :], 0), axis=1)
    return (blocks // seq_count, blocks * BLK + row_index % BLK)


def over_blocks(running, portions, step_fn):
    row_count = portions[0].shape[1]
    step_rows = math.gcd(row_count, 512)

    def advance(number, inner_carry):
        slabs = tuple(
            (
                lax.dynamic_slice_in_dim(portion, number * step_rows, step_rows, 1)
                for portion in portions
            )
        )
        return step_fn(inner_carry, slabs, number * step_rows)

    return lax.fori_loop(0, row_count // step_rows, advance, running)


def per_device(queries, keys, block_pos, query_map, key_map):
    local_q, local_k = (
        lax.all_to_all(queries, "head", split_axis=1, concat_axis=0, tiled=True),
        lax.all_to_all(keys, "head", split_axis=1, concat_axis=0, tiled=True),
    )
    seq_count = lax.axis_size("seq")
    seq_rank = lax.axis_index("seq")
    rows_local = local_k.shape[0]
    token_count = rows_local * seq_count
    key_heads = key_map.shape[0]
    group_width = query_map.shape[0] // key_heads
    score_scale = HEAD_SIZE ** (-0.5)
    query_index = seq_rank * rows_local + jnp.arange(rows_local, dtype=jnp.int32)
    query_heads = local_q.reshape(rows_local, key_heads, group_width, HEAD_SIZE).transpose(
        1, 2, 0, 3
    )
    query_wide = query_heads.astype(jnp.float32)
    query_logits = jnp.einsum(
        "vgnd,vgde->vgne",
        query_wide,
        query_map.reshape(key_heads, group_width, HEAD_SIZE, HEAD_SIZE),
        precision=HIGHEST,
    )
    rows_all = group_width * rows_local
    phi_query = softmax_pair(query_logits).reshape(key_heads, rows_all, 2 * HEAD_SIZE)
    phi_query_b = phi_query.astype(jnp.bfloat16)
    query_flat = query_heads.reshape(key_heads, rows_all, HEAD_SIZE)
    query_seq, query_at = row_places(query_index, block_pos, seq_count)
    query_seq = jnp.tile(query_seq, group_width)
    query_at = jnp.tile(query_at, group_width)

    def visible_for(offset, slab_rows):
        key_index = offset + jnp.arange(slab_rows, dtype=jnp.int32)
        key_seq, key_at = row_places(key_index, block_pos, seq_count)
        return (key_seq[None, :] == query_seq[:, None]) & (key_at[None, :] <= query_at[:, None])

    def key_features(key_slab):
        logits = jnp.einsum(
            "vwd,vde->vwe", key_slab.astype(jnp.float32), key_map, precision=HIGHEST
        )
        return softmax_pair(logits)

    def teacher(key_slab):
        return (
            jnp.einsum("vrd,vwd->vrw", query_flat, key_slab, preferred_element_type=jnp.float32)
            * score_scale
        )

    def stats_step(running, slabs, offset):
        key_slab = slabs[0]
        visible = visible_for(offset, key_slab.shape[1])

        def stats_compute_live(current):
            highest, denominator, linear_sum = current
            masked = jnp.where(visible[None], teacher(key_slab), NEG_FLOOR)
            new_high = jnp.maximum(highest, jnp.max(masked, axis=-1))
            exponent = jnp.where(visible[None], jnp.exp(masked - new_high[..., None]), 0.0)
            denominator = denominator * jnp.exp(highest - new_high) + jnp.sum(exponent, axis=-1)
            phi_key_b = slabs[1]
            linear = jnp.einsum(
                "vrf,vwf->vrw", phi_query_b, phi_key_b, preferred_element_type=jnp.float32
            )
            linear_sum = linear_sum + jnp.sum(jnp.where(visible[None], linear, 0.0), axis=-1)
            return (new_high, denominator, linear_sum)

        return lax.cond(jnp.any(visible), stats_compute_live, lambda current: current, running)

    def grads_step(running, slabs, offset):
        key_slab = slabs[0]
        visible = visible_for(offset, key_slab.shape[1])

        def grads_compute_live(current):
            query_grad, key_weight_grad = current
            masked = jnp.where(visible[None], teacher(key_slab), NEG_FLOOR)
            exponent = jnp.where(visible[None], jnp.exp(masked - highest[..., None]), 0.0)
            teacher_prob = exponent / denominator[..., None]
            phi_key = key_features(key_slab)
            phi_key_b = phi_key.astype(jnp.bfloat16)
            linear = jnp.einsum(
                "vrf,vwf->vrw", phi_query_b, phi_key_b, preferred_element_type=jnp.float32
            )
            weights = (
                jnp.where(visible[None], 1.0 / linear_sum[..., None] - teacher_prob / linear, 0.0)
                / token_count
            ).astype(jnp.bfloat16)
            query_grad = query_grad + jnp.einsum(
                "vrw,vwf->vrf", weights, phi_key_b, preferred_element_type=jnp.float32
            )
            key_grad = jnp.einsum(
                "vrw,vrf->vwf", weights, phi_query_b, preferred_element_type=jnp.float32
            )
            key_logit_grad = feature_grad(phi_key, key_grad)
            key_weight_grad = key_weight_grad + jnp.einsum(
                "vwd,vwe->vde", key_slab.astype(jnp.float32), key_logit_grad, precision=HIGHEST
            )
            return (query_grad, key_weight_grad)

        return lax.cond(jnp.any(visible), grads_compute_live, lambda current: current, running)

    def as_heads(pieces):
        return pieces.reshape(pieces.shape[0], key_heads, -1).transpose(1, 0, 2)

    row_zeros = jnp.zeros((key_heads, rows_all), jnp.float32)
    stats_init = (jnp.full((key_heads, rows_all), NEG_FLOOR, jnp.float32), row_zeros, row_zeros)
    grads_init = (
        jnp.zeros((key_heads, rows_all, 2 * HEAD_SIZE), jnp.float32),
        jnp.zeros((key_heads, HEAD_SIZE, HEAD_SIZE), jnp.float32),
    )
    local_features = key_features(as_heads(local_k)).astype(jnp.bfloat16)
    local_features = local_features.transpose(1, 0, 2).reshape(
        rows_local, key_heads * 2 * HEAD_SIZE
    )
    every_key, every_feature = sent_together((local_k, local_features), "seq", 0, 1)
    key_slabs = as_heads(every_key)
    highest, denominator, linear_sum = over_blocks(
        stats_init, (key_slabs, as_heads(every_feature)), stats_step
    )
    query_grad, key_weight_grad = over_blocks(grads_init, (key_slabs,), grads_step)
    query_logit_grad = feature_grad(phi_query, query_grad).reshape(
        key_heads, group_width, rows_local, HEAD_SIZE
    )
    query_weight_grad = jnp.einsum(
        "vgnd,vgne->vgde", query_wide, query_logit_grad, precision=HIGHEST
    ).reshape(key_heads * group_width, HEAD_SIZE, HEAD_SIZE)
    query_map_gradient, key_map_gradient = together((query_weight_grad, key_weight_grad), "seq")
    return (query_map_gradient, key_map_gradient)


def solution(mesh):
    in_specs = (
        P(("seq", "head"), None),
        P(("seq", "head"), None),
        P(),
        P("head", None, None),
        P("head", None, None),
    )
    out_specs = (P("head", None, None), P("head", None, None))
    return jax.shard_map(
        per_device, mesh=mesh, in_specs=in_specs, out_specs=out_specs, check_vma=False
    )
```

profile of v0, /device:TPU:32, one launch (start us, length us, event | category | flops | bytes accessed | tf_op | source)
XLA Modules:
  0.0 518.5 jit_solution(17320875823722990742)
XLA Ops:
  8.1 15.7 %all_to_all.50 = bf16[32,8,128]{2,0,1:T(8,128)(2,1)S(1)} all-to-all(bf16[32,8,128]{2,0,1:T(8,128)(2,1)S(1)} %copy_bitcast_fusion.1), channel_id=1, replica_groups=mesh['seq'=32,'head'=8] {'head'}, dimensions={1} | all-to-all | bytes 131072 | tf_op jit(solution)/shard_map/all_to_all | solution.py:110
  31.1 14.1 %all-to-all-done = bf16[32,8,512]{2,0,1:T(8,128)(2,1)S(1)} async-done(((bf16[32,8,512]{2,0,1:T(8,128)(2,1)}), bf16[32,8,512]{2,0,1:T(8,128)(2,1)S(1)}, u32[]{:S(2)}, u32[]{:S(2)}) %all-to-all-start) | async-done | bytes 262176 | tf_op jit(solution)/shard_map/all_to_all | solution.py:109
  47.3 162.8 %all-gather.2.cloned.1.call-done = bf16[8192,384]{0,1:T(8,128)(2,1)} async-done(((bf16[256,384]{0,1:T(8,128)(2,1)}), bf16[8192,384]{0,1:T(8,128)(2,1)}) %all-gather.2.cloned.1.call-update) | async-done | bytes 6291472 | tf_op jit(solution)/shard_map/all_gather | solution.py:19
  214.3 4.7 slice_bitcast_fusion
  219.0 6.4 %copy.52 = bf16[1,8192,256]{2,1,0:T(8,128)(2,1)} copy(bf16[1,8192,256]{1,2,0:T(8,128)(2,1)} %slice_bitcast_fusion) | data formatting | bytes 8388608
  225.4 83.3 %while.40 = (s32[]{:T(128)}, f32[1,1024]{1,0:T(1,128)S(1)}, f32[1,1024]{1,0:T(1,128)S(1)}, f32[1,1024]{1,0:T(1,128)S(1)}, s32[64]{0:T(128)S(1)}, /*index=5*/bf16...) while((s32[]{:T(128)}, f32[1,1024]{1,0:T(1,128)S(1)}, ...), condition=%wide.region_17.18_spmd.clone, body=%wide.region_9.17_spmd.clone.sunk | while | flops 410116096 | bytes 7592513 | solution.py:104
  252.1 3.6 conditional.6
  309.4 150.1 %while.41 = (s32[]{:T(128)}, f32[1,1024,256]{2,1,0:T(8,128)S(1)}, f32[1,128,128]{2,1,0:T(8,128)S(1)}, s32[64]{0:T(128)}, f32[1,1024]{1,0:T(1,128)S(1)}, /*index=...) while((s32[]{:T(128)}, f32[1,1024,256]{2,1,0:T(8,128)S(1)}, ...), condition=%wide.region_29.30_spmd.clone, body=%wide.region_18.29_spmd.clone.sunk | while | flops 1151864832 | bytes 16173653 | solution.py:104
  312.9 6.7 %conditional.7 = ((f32[1,1024,256]{2,1,0:T(8,128)S(1)}, f32[1,128,128]{2,1,0:T(8,128)S(1)})) conditional(s32[]{:T(128)} %convert_element_type.56, (f32[1,1024,256]{2,1,0:T(8,128)S(1)}, f32[1,128,128]{2,1,0:T(8,128)S(1)}) %tuple.166, (f32[1,1024]{1,0:T(1,128)S(1)}, s32[]{:T(128)}, bf16[1,8192,128]{2,1,0:T(8,128)(2,1)}, ...), branch_computations={%region_21.21_spmd, %region_22.28_spmd} | conditional | flops 1149646848 | bytes 15597638 | solution.py:204
  323.2 6.7 %conditional.7 = ((f32[1,1024,256]{2,1,0:T(8,128)S(1)}, f32[1,128,128]{2,1,0:T(8,128)S(1)})) conditional(s32[]{:T(128)} %convert_element_type.56, (f32[1,1024,256]{2,1,0:T(8,128)S(1)}, f32[1,128,128]{2,1,0:T(8,128)S(1)}) %tuple.166, (f32[1,1024]{1,0:T(1,128)S(1)}, s32[]{:T(128)}, bf16[1,8192,128]{2,1,0:T(8,128)(2,1)}, ...), branch_computations={%region_21.21_spmd, %region_22.28_spmd} | conditional | flops 1149646848 | bytes 15597638 | solution.py:204
  336.9 6.7 %conditional.7 = ((f32[1,1024,256]{2,1,0:T(8,128)S(1)}, f32[1,128,128]{2,1,0:T(8,128)S(1)})) conditional(s32[]{:T(128)} %convert_element_type.56, (f32[1,1024,256]{2,1,0:T(8,128)S(1)}, f32[1,128,128]{2,1,0:T(8,128)S(1)}) %tuple.166, (f32[1,1024]{1,0:T(1,128)S(1)}, s32[]{:T(128)}, bf16[1,8192,128]{2,1,0:T(8,128)(2,1)}, ...), branch_computations={%region_21.21_spmd, %region_22.28_spmd} | conditional | flops 1149646848 | bytes 15597638 | solution.py:204
  347.1 6.7 %conditional.7 = ((f32[1,1024,256]{2,1,0:T(8,128)S(1)}, f32[1,128,128]{2,1,0:T(8,128)S(1)})) conditional(s32[]{:T(128)} %convert_element_type.56, (f32[1,1024,256]{2,1,0:T(8,128)S(1)}, f32[1,128,128]{2,1,0:T(8,128)S(1)}) %tuple.166, (f32[1,1024]{1,0:T(1,128)S(1)}, s32[]{:T(128)}, bf16[1,8192,128]{2,1,0:T(8,128)(2,1)}, ...), branch_computations={%region_21.21_spmd, %region_22.28_spmd} | conditional | flops 1149646848 | bytes 15597638 | solution.py:204
  357.3 6.7 %conditional.7 = ((f32[1,1024,256]{2,1,0:T(8,128)S(1)}, f32[1,128,128]{2,1,0:T(8,128)S(1)})) conditional(s32[]{:T(128)} %convert_element_type.56, (f32[1,1024,256]{2,1,0:T(8,128)S(1)}, f32[1,128,128]{2,1,0:T(8,128)S(1)}) %tuple.166, (f32[1,1024]{1,0:T(1,128)S(1)}, s32[]{:T(128)}, bf16[1,8192,128]{2,1,0:T(8,128)(2,1)}, ...), branch_computations={%region_21.21_spmd, %region_22.28_spmd} | conditional | flops 1149646848 | bytes 15597638 | solution.py:204
  367.5 6.7 %conditional.7 = ((f32[1,1024,256]{2,1,0:T(8,128)S(1)}, f32[1,128,128]{2,1,0:T(8,128)S(1)})) conditional(s32[]{:T(128)} %convert_element_type.56, (f32[1,1024,256]{2,1,0:T(8,128)S(1)}, f32[1,128,128]{2,1,0:T(8,128)S(1)}) %tuple.166, (f32[1,1024]{1,0:T(1,128)S(1)}, s32[]{:T(128)}, bf16[1,8192,128]{2,1,0:T(8,128)(2,1)}, ...), branch_computations={%region_21.21_spmd, %region_22.28_spmd} | conditional | flops 1149646848 | bytes 15597638 | solution.py:204
  381.3 6.7 %conditional.7 = ((f32[1,1024,256]{2,1,0:T(8,128)S(1)}, f32[1,128,128]{2,1,0:T(8,128)S(1)})) conditional(s32[]{:T(128)} %convert_element_type.56, (f32[1,1024,256]{2,1,0:T(8,128)S(1)}, f32[1,128,128]{2,1,0:T(8,128)S(1)}) %tuple.166, (f32[1,1024]{1,0:T(1,128)S(1)}, s32[]{:T(128)}, bf16[1,8192,128]{2,1,0:T(8,128)(2,1)}, ...), branch_computations={%region_21.21_spmd, %region_22.28_spmd} | conditional | flops 1149646848 | bytes 15597638 | solution.py:204
  391.5 6.7 %conditional.7 = ((f32[1,1024,256]{2,1,0:T(8,128)S(1)}, f32[1,128,128]{2,1,0:T(8,128)S(1)})) conditional(s32[]{:T(128)} %convert_element_type.56, (f32[1,1024,256]{2,1,0:T(8,128)S(1)}, f32[1,128,128]{2,1,0:T(8,128)S(1)}) %tuple.166, (f32[1,1024]{1,0:T(1,128)S(1)}, s32[]{:T(128)}, bf16[1,8192,128]{2,1,0:T(8,128)(2,1)}, ...), branch_computations={%region_21.21_spmd, %region_22.28_spmd} | conditional | flops 1149646848 | bytes 15597638 | solution.py:204
  401.7 6.7 %conditional.7 = ((f32[1,1024,256]{2,1,0:T(8,128)S(1)}, f32[1,128,128]{2,1,0:T(8,128)S(1)})) conditional(s32[]{:T(128)} %convert_element_type.56, (f32[1,1024,256]{2,1,0:T(8,128)S(1)}, f32[1,128,128]{2,1,0:T(8,128)S(1)}) %tuple.166, (f32[1,1024]{1,0:T(1,128)S(1)}, s32[]{:T(128)}, bf16[1,8192,128]{2,1,0:T(8,128)(2,1)}, ...), branch_computations={%region_21.21_spmd, %region_22.28_spmd} | conditional | flops 1149646848 | bytes 15597638 | solution.py:204
  411.9 6.7 %conditional.7 = ((f32[1,1024,256]{2,1,0:T(8,128)S(1)}, f32[1,128,128]{2,1,0:T(8,128)S(1)})) conditional(s32[]{:T(128)} %convert_element_type.56, (f32[1,1024,256]{2,1,0:T(8,128)S(1)}, f32[1,128,128]{2,1,0:T(8,128)S(1)}) %tuple.166, (f32[1,1024]{1,0:T(1,128)S(1)}, s32[]{:T(128)}, bf16[1,8192,128]{2,1,0:T(8,128)(2,1)}, ...), branch_computations={%region_21.21_spmd, %region_22.28_spmd} | conditional | flops 1149646848 | bytes 15597638 | solution.py:204
  422.1 6.7 %conditional.7 = ((f32[1,1024,256]{2,1,0:T(8,128)S(1)}, f32[1,128,128]{2,1,0:T(8,128)S(1)})) conditional(s32[]{:T(128)} %convert_element_type.56, (f32[1,1024,256]{2,1,0:T(8,128)S(1)}, f32[1,128,128]{2,1,0:T(8,128)S(1)}) %tuple.166, (f32[1,1024]{1,0:T(1,128)S(1)}, s32[]{:T(128)}, bf16[1,8192,128]{2,1,0:T(8,128)(2,1)}, ...), branch_computations={%region_21.21_spmd, %region_22.28_spmd} | conditional | flops 1149646848 | bytes 15597638 | solution.py:204
  432.4 6.7 %conditional.7 = ((f32[1,1024,256]{2,1,0:T(8,128)S(1)}, f32[1,128,128]{2,1,0:T(8,128)S(1)})) conditional(s32[]{:T(128)} %convert_element_type.56, (f32[1,1024,256]{2,1,0:T(8,128)S(1)}, f32[1,128,128]{2,1,0:T(8,128)S(1)}) %tuple.166, (f32[1,1024]{1,0:T(1,128)S(1)}, s32[]{:T(128)}, bf16[1,8192,128]{2,1,0:T(8,128)(2,1)}, ...), branch_computations={%region_21.21_spmd, %region_22.28_spmd} | conditional | flops 1149646848 | bytes 15597638 | solution.py:204
  442.6 6.7 %conditional.7 = ((f32[1,1024,256]{2,1,0:T(8,128)S(1)}, f32[1,128,128]{2,1,0:T(8,128)S(1)})) conditional(s32[]{:T(128)} %convert_element_type.56, (f32[1,1024,256]{2,1,0:T(8,128)S(1)}, f32[1,128,128]{2,1,0:T(8,128)S(1)}) %tuple.166, (f32[1,1024]{1,0:T(1,128)S(1)}, s32[]{:T(128)}, bf16[1,8192,128]{2,1,0:T(8,128)(2,1)}, ...), branch_computations={%region_21.21_spmd, %region_22.28_spmd} | conditional | flops 1149646848 | bytes 15597638 | solution.py:204
  452.8 6.7 %conditional.7 = ((f32[1,1024,256]{2,1,0:T(8,128)S(1)}, f32[1,128,128]{2,1,0:T(8,128)S(1)})) conditional(s32[]{:T(128)} %convert_element_type.56, (f32[1,1024,256]{2,1,0:T(8,128)S(1)}, f32[1,128,128]{2,1,0:T(8,128)S(1)}) %tuple.166, (f32[1,1024]{1,0:T(1,128)S(1)}, s32[]{:T(128)}, bf16[1,8192,128]{2,1,0:T(8,128)(2,1)}, ...), branch_computations={%region_21.21_spmd, %region_22.28_spmd} | conditional | flops 1149646848 | bytes 15597638 | solution.py:204
  462.1 34.5 %all_to_all.52 = f32[32,1,2560]{2,1,0:T(1,128)S(1)} all-to-all(f32[32,1,2560]{2,1,0:T(1,128)S(1)} %bitcast.205), channel_id=1, replica_groups=mesh['seq'=32,'head'=8] {'seq'}, dimensions={0} | all-to-all | bytes 655360 | tf_op jit(solution)/shard_map/all_to_all | solution.py:50
  497.0 13.3 %all_to_all.51 = f32[32,1,2560]{2,1,0:T(1,128)S(1)} all-to-all(f32[32,1,2560]{2,1,0:T(1,128)S(1)} %broadcast_in_dim.167), channel_id=1, replica_groups=mesh['seq'=32,'head'=8] {'seq'}, dimensions={0} | all-to-all | bytes 655360 | tf_op jit(solution)/shard_map/all_to_all | solution.py:36
  (531 shorter events, 274.7 us)
Async XLA Ops:
  7.2 38.2 %copy-start = (f32[4,128,128]{2,1,0:T(8,128)S(1)}, f32[4,128,128]{2,1,0:T(8,128)}, u32[]{:S(2)}) copy-start(f32[4,128,128]{2,1,0:T(8,128)} %param.16) | copy-start | bytes 786436
  7.2 23.8 %copy-start.7 = (s32[64]{0:T(128)S(1)}, s32[64]{0:T(128)}, u32[]{:S(2)}) copy-start(s32[64]{0:T(128)} %param.15) | copy-start | bytes 772
  7.2 202.9 %all-gather.2.cloned.1.call-start = ((), (), s32[]{:S(2)}) async-start(), calls=%async_computation.4 | async-start | bytes 6488064 | tf_op jit(solution)/shard_map/all_gather | solution.py:19
  27.6 17.6 %all-to-all-start = ((bf16[32,8,512]{2,0,1:T(8,128)(2,1)}), bf16[32,8,512]{2,0,1:T(8,128)(2,1)S(1)}, u32[]{:S(2)}, u32[]{:S(2)}) async-start(bf16[32,8,512]{2,0,1:T(8,128)(2,1)} %bitcast.179), calls=%async_computation | async-start | bytes 524288 | tf_op jit(solution)/shard_map/all_to_all | solution.py:109
  46.1 0.8 copy-start.1
  46.4 0.8 copy-start.3
  225.4 84.0 %copy-start.5 = (f32[1,128,128]{2,1,0:T(8,128)S(1)}, f32[1,128,128]{2,1,0:T(8,128)}, u32[]{:S(2)}) copy-start(f32[1,128,128]{2,1,0:T(8,128)} %param.17) | copy-start | bytes 196612
  308.7 0.6 copy-start.6
  309.4 150.1 %copy-start.2 = (f32[4,256,128]{2,1,0:T(8,128)S(1)}, f32[4,256,128]{2,1,0:T(8,128)}, u32[]{:S(2)}) copy-start(f32[4,256,128]{2,1,0:T(8,128)} %copy-done.1) | copy-start | bytes 1572868
  459.5 1.5 copy-start.4
Sparse Core Ops, SparseCore 0:
  26.0 184.0 all-gather.1
where the time goes:
time: 521 us; the launch traced here: 518 us
  waiting for transfers between devices  177 us (34%)
  matrix products  130 us (25%)
  other arithmetic  73.7 us (14%)
  blocking collectives  63.4 us (12%)
  local copies, waits for them, and re-layouts  32.3 us (6%)
  loops' own time  24.7 us (5%)
  between operations  14.3 us (3%)
    all_gather x1, waiting for transfers between devices, sent_together(): whole = lax.all_gather(both, axis, axis=dim, tiled=True)  163 us
    dot_general x28, matrix products, teacher(): jnp.einsum('vrd,vwd->vrw', query_flat, key_slab, preferred_element_type=j...  38.6 us
    all_to_all x1, blocking collectives, summed_on_arrival(): parts = lax.all_to_all(split_up(value, dim, count), axis, 0, 0, tiled=True)  34.5 us
    another operation x2, loops' own time, over_blocks(): return lax.fori_loop(0, row_count // step_rows, advance, running)  22.6 us
    reduce_or x16, other arithmetic, grads_step(): jnp.any(visible)  21.2 us
    reduce_or x16, other arithmetic, stats_step(): jnp.any(visible)  20.1 us
    dot_general x14, matrix products, stats_compute_live(): jnp.einsum('vrf,vwf->vrw', phi_query_b, phi_key_b, preferred_element_type...  20.1 us
    dot_general x14, matrix products, grads_compute_live(): jnp.einsum('vwd,vwe->vde', key_slab.astype(jnp.float32), key_logit_grad,...  18.9 us
  transfers between devices with their start and end apart: 2, of which 2 were waited for; matrix products, arithmetic and copies ran while one was open for 1% of the time, Pallas kernels for 0%

commit v1 on v0

v1 whole, which is shorter than its diff:
```python
import functools
import math

import jax
import jax.numpy as jnp
from jax import lax
from jax.experimental import pallas as pl
from jax.experimental.pallas import tpu as pltpu
from jax.sharding import PartitionSpec as P

MESH = pl.DeviceIdType.MESH
BF16 = jnp.bfloat16
F32 = jnp.float32
NEG = -1e30
TOKENS = 8192
SCALE = 128 ** (-0.5)
EXP2_SCALE = SCALE * math.log2(math.e)


def place():
    s, h = lax.axis_index("seq"), lax.axis_index("head")
    y, x, zl = s // 8, (s // 2) % 4, s % 2
    zh, c = h // 2, h % 2
    return y, x, zh, zl, c


def device(y, x, z, c):
    return {"seq": (y * 4 + x) * 2 + z % 2, "head": (z // 2) * 2 + c}


class Copies:
    def __init__(self, send, recv):
        self.send, self.recv, self.count = send, recv, 0
        self.started = []

    def start(self, src, dst, to):
        copy = pltpu.make_async_remote_copy(
            src_ref=src, dst_ref=dst, send_sem=self.send.at[self.count],
            recv_sem=self.recv.at[self.count], device_id=to, device_id_type=MESH)
        self.count += 1
        copy.start()
        self.started.append(copy)
        return copy

    def finish(self):
        for copy in self.started:
            copy.wait_send()


EXCHANGE_COPIES = 112


def exchange_kernel(q_ref, k_ref, wq_ref, wk_ref, qall, kall, wqr, wkr, landed, send, recv):
    y, x, zh, zl, c = place()
    z = zh * 2 + zl
    b, z2 = zl * 2 + zh // 2, zh % 2
    quarter = z2 * 2 + c
    net = Copies(send, recv)

    def cols(block, width):
        return pl.ds(pl.multiple_of(block * width, width), width)

    kall[y, x, b, z2, c] = k_ref[:, cols(z, 128)]
    landed[quarter, b] = q_ref[pl.ds(pl.multiple_of(c * 16, 16), 16), cols(z, 512)]

    barrier = pltpu.get_barrier_semaphore()
    for dz in range(8):
        for dc in range(2):
            if dz or dc:
                pl.semaphore_signal(barrier, inc=1, device_id=device(y, x, (z + dz) % 8, (c + dc) % 2), device_id_type=MESH)
    for dy in range(4):
        for dx in range(4):
            if dy or dx:
                pl.semaphore_signal(barrier, inc=1, device_id=device((y + dy) % 4, (x + dx) % 4, z, c), device_id_type=MESH)
    pl.semaphore_wait(barrier, 30)

    partner = device(y, x, z, 1 - c)
    k_first = []
    for dz in (4, 3, 5, 2, 6, 1, 7):
        to = (z + dz) % 8
        k_first.append(net.start(k_ref.at[:, cols(to, 128)], kall.at[y, x, b, z2, c], device(y, x, to, c)))
    q_first = []
    for dz in (4, 3, 5, 2, 6, 1, 7, 0):
        for dc in range(2):
            if dz or dc:
                to, core = (z + dz) % 8, (c + dc) % 2
                q_first.append(net.start(
                    q_ref.at[pl.ds(pl.multiple_of(core * 16, 16), 16), cols(to, 512)],
                    landed.at[quarter, b], device(y, x, to, core)))
    maps = [net.start(wq_ref.at[y], wqr, partner), net.start(wk_ref.at[0], wkr, partner)]

    def piece(y0, x0, half):
        return kall.at[y0, x0, pl.ds(2 * half, 2), :, c]

    for copy in k_first:
        copy.wait_recv()
    direct = {}
    for d in (2, 1, 3):
        for half in range(2):
            src = piece(y, x, half)
            direct[half, 0, d] = net.start(src, src, device(y, (x + d) % 4, z, c))
            direct[half, d, 0] = net.start(src, src, device((y + d) % 4, x, z, c))
    shared = []
    for half in range(2):
        src = piece(y, x, half)
        shared.append(net.start(src, src, partner))
    relayed = {}
    for d in (1, 3, 2):
        direct[0, 0, d].wait_recv()
        src = piece(y, (x - d) % 4, 0)
        for e in (2, 1, 3):
            relayed[0, e, d] = net.start(src, src, device((y + e) % 4, x, z, c))
        shared.append(net.start(src, src, partner))
        direct[1, d, 0].wait_recv()
        src = piece((y - d) % 4, x, 1)
        for e in (2, 1, 3):
            relayed[1, d, e] = net.start(src, src, device(y, (x + e) % 4, z, c))
        shared.append(net.start(src, src, partner))
    for d in (1, 3, 2):
        direct[1, 0, d].wait_recv()
        src = piece(y, (x - d) % 4, 1)
        shared.append(net.start(src, src, partner))
        direct[0, d, 0].wait_recv()
        src = piece((y - d) % 4, x, 0)
        shared.append(net.start(src, src, partner))

    for copy in q_first:
        copy.wait_recv()
    q_second = []
    for dy in (2, 1, 3, 0):
        for dx in (2, 1, 3, 0):
            if dy or dx:
                y1, x1 = (y + dy) % 4, (x + dx) % 4
                q_second.append(net.start(
                    landed.at[x1, :, :, cols(y1, 128)], qall.at[y * 4 + x], device(y1, x1, z, c)))
    qall[y * 4 + x] = landed[x, :, :, cols(y, 128)]

    for dx in (1, 3, 2):
        for dy in (1, 3, 2):
            for half in range(2):
                relayed[half, dy, dx].wait_recv()
                src = piece((y - dy) % 4, (x - dx) % 4, half)
                shared.append(net.start(src, src, partner))
    for copy in maps + q_second + shared:
        copy.wait_recv()
    net.finish()


def exchange(queries, keys, query_map, key_map):
    vmem = pl.BlockSpec(memory_space=pltpu.VMEM)
    return pl.pallas_call(
        exchange_kernel,
        out_shape=(
            jax.ShapeDtypeStruct((16, 4, 16, 128), BF16),
            jax.ShapeDtypeStruct((4, 4, 4, 2, 2, 32, 128), BF16),
            jax.ShapeDtypeStruct((128, 128), F32),
            jax.ShapeDtypeStruct((128, 128), F32),
        ),
        in_specs=[vmem] * 4,
        out_specs=(vmem,) * 4,
        scratch_shapes=[
            pltpu.VMEM((4, 4, 16, 512), BF16),
            pltpu.SemaphoreType.DMA((EXCHANGE_COPIES,)),
            pltpu.SemaphoreType.DMA((EXCHANGE_COPIES,)),
        ],
        compiler_params=pltpu.CompilerParams(collective_id=0, has_side_effects=True),
        name="exchange",
    )(queries, keys, query_map, key_map)


def dot_nt(a, b):
    return lax.dot_general(a, b, (((1,), (1,)), ((), ())), preferred_element_type=F32)


def dot_nn(a, b):
    return lax.dot_general(a, b, (((1,), (0,)), ((), ())), preferred_element_type=F32)


def split3(a):
    hi = a.astype(BF16)
    rest = a - hi.astype(F32)
    mid = rest.astype(BF16)
    lo = (rest - mid.astype(F32)).astype(BF16)
    return jnp.concatenate([hi, mid, lo], axis=0)


def add3(p):
    return p[:128] + (p[128:256] + p[256:])


def softmax_pair_t(logits):
    up = jnp.exp(logits - jnp.max(logits, axis=0, keepdims=True))
    down = jnp.exp(jnp.min(logits, axis=0, keepdims=True) - logits)
    up = up * (1.0 / jnp.sum(up, axis=0, keepdims=True))
    down = down * (1.0 / jnp.sum(down, axis=0, keepdims=True))
    return up, down


def feature_grad_t(up, down, grad):
    grad_up, grad_down = grad[:128], grad[128:]
    first = up * (grad_up - jnp.sum(grad_up * up, axis=0, keepdims=True))
    second = down * (grad_down - jnp.sum(grad_down * down, axis=0, keepdims=True))
    return first - second


CH = 512


def compute_kernel(inv, q_ref, k_ref, wq_own, wq_got, wk_own, wk_got, out_q, out_k,
                   wq3, wk3, qs, ks, kf, kb, qf, qtb, qb, t_ref, s_ref, w_ref, gq, acc_q, acc_k):
    y, x, zh, zl, c = place()
    own = zl == c

    @pl.when(own)
    def _():
        wq3[...] = split3(wq_own[y].T)
        wk3[...] = split3(wk_own[0].T)

    @pl.when(jnp.logical_not(own))
    def _():
        wq3[...] = split3(wq_got[...].T)
        wk3[...] = split3(wk_got[...].T)

    acc_q[...] = jnp.zeros_like(acc_q)
    acc_k[...] = jnp.zeros_like(acc_k)
    first_row = (2 * x + c) * 16
    row = lax.broadcasted_iota(jnp.int32, (128, CH), 0)
    last_live = (row // 16) * 128 + row % 16 + first_row
    key = lax.broadcasted_iota(jnp.int32, (128, CH), 1)

    def live(j):
        return key + j * CH <= last_live

    def one_sequence(number, carry):
        def gather(p, inner):
            stored = inv[number * 32 + p]
            qs[pl.ds(pl.multiple_of(p * 16, 16), 16), :] = q_ref[stored]
            ks[pl.ds(pl.multiple_of(p * 128, 128), 128), :] = k_ref[stored]
            return inner

        lax.fori_loop(0, 32, gather, 0)

        def key_features(j, inner):
            at = pl.multiple_of(j * CH, CH)
            up, down = softmax_pair_t(add3(dot_nt(wk3[...], ks[pl.ds(at, CH), :])))
            kf[0:128, pl.ds(at, CH)] = up
            kf[128:256, pl.ds(at, CH)] = down
            kb[0:128, pl.ds(at, CH)] = up.astype(BF16)
            kb[128:256, pl.ds(at, CH)] = down.astype(BF16)
            return inner

        lax.fori_loop(0, 4096 // CH, key_features, 0)
        up, down = softmax_pair_t(add3(dot_nt(wq3[...], qs[...])))
        qf[0:128] = up
        qf[128:256] = down
        qtb[0:128] = up.astype(BF16)
        qtb[128:256] = down.astype(BF16)
        qb[:, 0:128] = up.T.astype(BF16)
        qb[:, 128:256] = down.T.astype(BF16)

        for r in range(4):
            rows = slice(128 * r, 128 * r + 128)
            per = 1024 // CH
            chunks = per * (r + 1)
            q_tile = qs[rows, :]
            phi_tile = qb[rows, :]
            high = jnp.full((128, 128), NEG, F32)
            for j in range(chunks):
                t = dot_nt(q_tile, ks[j * CH:(j + 1) * CH, :])
                if j >= per * r:
                    t = jnp.where(live(j - per * r), t, NEG)
                t_ref[:, j * CH:(j + 1) * CH] = t
                for k in range(CH // 128):
                    high = jnp.maximum(high, t[:, k * 128:(k + 1) * 128])
            high = jnp.max(high, axis=1, keepdims=True)
            den = jnp.zeros((128, 128), F32)
            lin = jnp.zeros((128, 128), F32)
            for j in range(chunks):
                e = jnp.exp2((t_ref[:, j * CH:(j + 1) * CH] - high) * EXP2_SCALE)
                t_ref[:, j * CH:(j + 1) * CH] = e
                s = dot_nn(phi_tile, kb[:, j * CH:(j + 1) * CH])
                s_ref[:, j * CH:(j + 1) * CH] = s
                if j >= per * r:
                    s = jnp.where(live(j - per * r), s, 0.0)
                for k in range(CH // 128):
                    den = den + e[:, k * 128:(k + 1) * 128]
                    lin = lin + s[:, k * 128:(k + 1) * 128]
            den = (1.0 / TOKENS) / jnp.sum(den, axis=1, keepdims=True)
            lin = (1.0 / TOKENS) / jnp.sum(lin, axis=1, keepdims=True)
            for j in range(chunks):
                cut = slice(j * CH, (j + 1) * CH)
                w = lin - (t_ref[:, cut] * den) / s_ref[:, cut]
                if j >= per * r:
                    w = jnp.where(live(j - per * r), w, 0.0)
                w_ref[rows, cut] = w.astype(BF16)
            n = 1024 * (r + 1)
            gq[rows, :] = dot_nt(w_ref[rows, 0:n], kb[:, 0:n])

        for j in range(4096 // CH):
            top = 128 * (j * CH // 1024)
            cut = slice(j * CH, (j + 1) * CH)
            grad = dot_nn(qtb[:, top:512], w_ref[top:512, cut])
            d = feature_grad_t(kf[0:128, cut], kf[128:256, cut], grad)
            acc_k[...] += add3(dot_nn(split3(d), ks[cut, :]))
        d = feature_grad_t(qf[0:128], qf[128:256], gq[...].T)
        acc_q[...] += add3(dot_nn(split3(d), qs[...]))
        return carry

    lax.fori_loop(0, 2, one_sequence, 0)
    out_q[...] = acc_q[...].T
    out_k[...] = acc_k[...].T


def compute(inv, q, k, wq_own, wq_got, wk_own, wk_got):
    vmem = pl.BlockSpec(memory_space=pltpu.VMEM)
    return pl.pallas_call(
        compute_kernel,
        out_shape=(jax.ShapeDtypeStruct((128, 128), F32),) * 2,
        in_specs=[pl.BlockSpec(memory_space=pltpu.SMEM)] + [vmem] * 6,
        out_specs=(vmem,) * 2,
        scratch_shapes=[
            pltpu.VMEM((384, 128), BF16),
            pltpu.VMEM((384, 128), BF16),
            pltpu.VMEM((512, 128), BF16),
            pltpu.VMEM((4096, 128), BF16),
            pltpu.VMEM((256, 4096), F32),
            pltpu.VMEM((256, 4096), BF16),
            pltpu.VMEM((256, 512), F32),
            pltpu.VMEM((256, 512), BF16),
            pltpu.VMEM((512, 256), BF16),
            pltpu.VMEM((128, 4096), F32),
            pltpu.VMEM((128, 4096), F32),
            pltpu.VMEM((512, 4096), BF16),
            pltpu.VMEM((512, 256), F32),
            pltpu.VMEM((128, 128), F32),
            pltpu.VMEM((128, 128), F32),
        ],
        name="compute",
    )(inv, q, k, wq_own, wq_got, wk_own, wk_got)


REDUCE_COPIES = 128


def reduce_kernel(pq, pk, out_q, out_k, got_q, got_k, sum_q, sum_k, send_q, recv_q, send_k, recv_k, bsend_q, brecv_q, bsend_k, brecv_k):
    y, x, zh, zl, c = place()
    z = zh * 2 + zl
    owner = c == zl
    other = zh * 2 + (1 - zl)

    barrier = pltpu.get_barrier_semaphore()
    for dy in range(4):
        for dx in range(4):
            for plane in range(2):
                for dc in range(2):
                    if dy or dx or plane or dc:
                        pl.semaphore_signal(
                            barrier, inc=1,
                            device_id=device((y + dy) % 4, (x + dx) % 4, zh * 2 + (zl + plane) % 2, (c + dc) % 2),
                            device_id_type=MESH)

    mine = 2 * x + c
    got_q[mine] = pq[pl.ds(pl.multiple_of(mine * 16, 16), 16), :]
    slot = y * 4 + x

    @pl.when(owner)
    def _():
        got_k[2 * slot + c] = pk[pl.ds(pl.multiple_of(slot * 8, 8), 8), :]

    pl.semaphore_wait(barrier, 63)

    def send_to(src, dst, sems, rsems, at, to):
        return pltpu.make_async_remote_copy(
            src_ref=src, dst_ref=dst, send_sem=sems.at[at], recv_sem=rsems.at[at], device_id=to, device_id_type=MESH)

    def k_copy(dy, dx, dc):
        y1, x1 = (y + dy) % 4, (x + dx) % 4
        at = ((dy * 4) + dx) * 2 + dc
        return send_to(pk.at[pl.ds(pl.multiple_of((y1 * 4 + x1) * 8, 8), 8), :], got_k.at[2 * slot + c],
                       send_k, recv_k, at, device(y1, x1, z, zl))

    def q_copy(dx, dc):
        x1, c1 = (x + dx) % 4, (c + dc) % 2
        return send_to(pq.at[pl.ds(pl.multiple_of((2 * x1 + c1) * 16, 16), 16), :], got_q.at[mine],
                       send_q, recv_q, dx * 2 + dc, device(y, x1, z, c1))

    far = [(dy, dx) for dy in (2, 1, 3, 0) for dx in (2, 1, 3, 0)]
    for dy, dx in far:
        if dy or dx:
            @pl.when(owner)
            def _(dy=dy, dx=dx):
                k_copy(dy, dx, 0).start()

            @pl.when(jnp.logical_not(owner))
            def _(dy=dy, dx=dx):
                k_copy(dy, dx, 1).start()
        else:
            @pl.when(jnp.logical_not(owner))
            def _():
                k_copy(0, 0, 1).start()
    for dx in (2, 1, 3, 0):
        for dc in range(2):
            if dx or dc:
                q_copy(dx, dc).start()

    for dx in (0, 1, 3, 2):
        for dc in range(2):
            if dx or dc:
                q_copy(dx, dc).wait_recv()
    total = got_q[0]
    for i in range(1, 8):
        total = total + got_q[i]
    sum_q[...] = total

    @pl.when(owner)
    def _():
        for dy, dx in far:
            for dc in range(2):
                if dy or dx or dc:
                    k_copy(dy, dx, dc).wait_recv()
        total = got_k[0]
        for i in range(1, 32):
            total = total + got_k[i]
        sum_k[...] = total

    rows_q = pl.ds(pl.multiple_of(mine * 16, 16), 16)
    rows_k = pl.ds(pl.multiple_of(slot * 8, 8), 8)

    def q_out(dy, dx, plane, core):
        to = zh * 2 + (zl + plane) % 2
        at = ((dy * 4 + dx) * 2 + plane) * 2 + core
        return send_to(sum_q, out_q.at[y, rows_q, :], bsend_q, brecv_q, at, device((y + dy) % 4, (x + dx) % 4, to, zl))

    def k_out(dy, dx, plane):
        to = zh * 2 + (zl + plane) % 2
        at = (dy * 4 + dx) * 2 + plane
        return send_to(sum_k, out_k.at[0, rows_k, :], bsend_k, brecv_k, at, device((y + dy) % 4, (x + dx) % 4, to, zl))

    def sends(act):
        for plane in (1, 0):
            for dy, dx in far:
                @pl.when(owner)
                def _(dy=dy, dx=dx, plane=plane):
                    if dy or dx or plane:
                        act(q_out(dy, dx, plane, 0))
                        act(k_out(dy, dx, plane))

                @pl.when(jnp.logical_not(owner))
                def _(dy=dy, dx=dx, plane=plane):
                    act(q_out(dy, dx, plane, 1))

    sends(lambda copy: copy.start())

    @pl.when(owner)
    def _():
        out_q[y, rows_q, :] = sum_q[...]
        out_k[0, rows_k, :] = sum_k[...]
        for dy, dx in far:
            for core in range(2):
                if dy or dx or core:
                    q_out(dy, dx, 0, core).wait_recv()
            if dy or dx:
                k_out(dy, dx, 0).wait_recv()

    @pl.when(jnp.logical_not(owner))
    def _():
        for dy, dx in far:
            for core in range(2):
                q_out(dy, dx, 1, core).wait_recv()
            k_out(dy, dx, 1).wait_recv()

    sends(lambda copy: copy.wait_send())
    for dy, dx in far:
        @pl.when(owner)
        def _(dy=dy, dx=dx):
            if dy or dx:
                k_copy(dy, dx, 0).wait_send()

        @pl.when(jnp.logical_not(owner))
        def _(dy=dy, dx=dx):
            k_copy(dy, dx, 1).wait_send()
    for dx in range(4):
        for dc in range(2):
            if dx or dc:
                q_copy(dx, dc).wait_send()


def reduce(pq, pk):
    vmem = pl.BlockSpec(memory_space=pltpu.VMEM)
    dma = pltpu.SemaphoreType.DMA
    return pl.pallas_call(
        reduce_kernel,
        out_shape=(jax.ShapeDtypeStruct((4, 128, 128), F32), jax.ShapeDtypeStruct((1, 128, 128), F32)),
        in_specs=[vmem] * 2,
        out_specs=(vmem,) * 2,
        scratch_shapes=[
            pltpu.VMEM((8, 16, 128), F32),
            pltpu.VMEM((32, 8, 128), F32),
            pltpu.VMEM((16, 128), F32),
            pltpu.VMEM((8, 128), F32),
            dma((8,)), dma((8,)), dma((32,)), dma((32,)),
            dma((64,)), dma((64,)), dma((32,)), dma((32,)),
        ],
        compiler_params=pltpu.CompilerParams(collective_id=1, has_side_effects=True),
        name="reduce",
    )(pq, pk)


def per_device(queries, keys, block_pos, query_map, key_map):
    order = jnp.arange(64, dtype=jnp.int32)
    inv = jnp.sum(jnp.where(block_pos[None, :] == order[:, None], order[None, :], 0), axis=1, dtype=jnp.int32)
    q, k, wq_got, wk_got = exchange(queries, keys, query_map, key_map)
    pq, pk = compute(inv, q.reshape(64, 16, 128), k.reshape(64, 128, 128), query_map, wq_got, key_map, wk_got)
    return reduce(pq, pk)


def solution(mesh):
    in_specs = (
        P(("seq", "head"), None),
        P(("seq", "head"), None),
        P(),
        P("head", None, None),
        P("head", None, None),
    )
    out_specs = (P("head", None, None), P("head", None, None))
    return jax.shard_map(
        per_device, mesh=mesh, in_specs=in_specs, out_specs=out_specs, check_vma=False
    )
```

time: 521 us -> 83.8 us (0.16)
  waiting for transfers between devices: 177 us -> 0 us
  matrix products: 130 us -> 0 us
  Pallas kernels: 0 us -> 77 us
  other arithmetic: 73.7 us -> 1.37 us
  blocking collectives: 63.4 us -> 0 us
  local copies, waits for them, and re-layouts: 32.3 us -> 3.14 us
  loops' own time: 24.7 us -> 0 us
  between operations: 14.3 us -> 0.65 us
    all_gather x1 -> x0, waiting for transfers between devices: 163 us -> none  [sent_together(): whole = lax.all_gather(both, axis, axis=dim, tiled=True)]
    dot_general x115 -> x0, matrix products: 130 us -> none  [the longest x28 38.6 us: teacher(): jnp.einsum('vrd,vwd->vrw', query_flat, key_slab, preferred_element_type=j...]
    pallas_call x0 -> x3, Pallas kernels: none -> 77 us  [the longest x1 32.4 us: exchange(): pl.pallas_call(exchange_kernel, out_shape=(jax.ShapeDtypeStruct((16, 4, 1...]
    all_to_all x3 -> x0, blocking collectives: 63.4 us -> none  [the longest x1 34.5 us: summed_on_arrival(): parts = lax.all_to_all(split_up(value, dim, count), axis, 0, 0, tiled=True)]
    reduce_or x32 -> x0, other arithmetic: 41.3 us -> none  [the longest x16 21.2 us: grads_step(): jnp.any(visible)]
    reduce_sum x78 -> x1, other arithmetic: 27.5 us -> 1.37 us  [per_device(): jnp.sum(jnp.where(block_pos[None, :] == order[:, None], order[None, :], 0...]
    another operation x34 -> x0, loops' own time: 24.7 us -> none  [the longest x2 22.6 us: over_blocks(): return lax.fori_loop(0, row_count // step_rows, advance, running)]
    all_to_all x1 -> x0, waiting for transfers between devices: 14.1 us -> none  [per_device(): lax.all_to_all(queries, 'head', split_axis=1, concat_axis=0, tiled=True)]
  transfers between devices with their start and end apart: 2 -> 0, of which waited for: 2 -> 0; matrix products, arithmetic and copies ran while one was open for 1% -> 0% of each run, Pallas kernels for 0% -> 0%
where the time goes in v1:
time: 83.8 us; the launch traced here: 82.2 us
  Pallas kernels  77 us (92%)
  local copies, waits for them, and re-layouts  3.14 us (4%)
  other arithmetic  1.37 us (2%)
    pallas_call x1, Pallas kernels, exchange(): pl.pallas_call(exchange_kernel, out_shape=(jax.ShapeDtypeStruct((16, 4, 1...  32.4 us
    pallas_call x1, Pallas kernels, compute(): pl.pallas_call(compute_kernel, out_shape=(jax.ShapeDtypeStruct((128, 128)...  26.1 us
    pallas_call x1, Pallas kernels, reduce(): pl.pallas_call(reduce_kernel, out_shape=(jax.ShapeDtypeStruct((4, 128, 12...  18.6 us
    unnamed x2, local copies, waits for them, and re-layouts  3.14 us

profile of v1, /device:TPU:32, one launch (start us, length us, event | category | flops | bytes accessed | tf_op | source)
XLA Modules:
  0.0 82.2 jit_solution(889817746631764314)
XLA Ops:
  0.6 1.4 %select_reduce_fusion.inv = s32[64]{0:T(128)} fusion(s32[64]{0:T(128)} %param.7), kind=kLoop, calls=%fused_computation | loop fusion | flops 12224 | bytes 512 | tf_op jit(solution)/shard_map/reduce_sum | solution.py:511
  2.0 32.4 %exchange.1 = (bf16[16,4,16,128]{3,2,1,0:T(8,128)(2,1)}, bf16[4,4,4,2,2,32,128]{6,5,4,3,2,1,0:T(8,128)(2,1)}, f32[128,128]{1,0:T(8,128)}, f32[128,128]{1,0:T(8,128)}) custom-call(bf16[32,4096]{1,0:T(8,128)(2,1)} %q_ref.1, bf16[32,1024]{1,0:T(8,128)(2,1)} %k_ref.1, f32[4,128,128]{2,1,0:T(8,128)} %wq_own.1, f32[1,128,128]{2,1,0:T(8,128)} %wk_own.1), custom_call_target="tpu_custom_call" | custom-call | tf_op jit(solution)/shard_map/exchange/pallas_call | solution.py:151
  34.4 26.1 %compute.1 = (f32[128,128]{1,0:T(8,128)}, f32[128,128]{1,0:T(8,128)}) custom-call(s32[64]{0:T(128)} %select_reduce_fusion.inv, bf16[64,16,128]{2,1,0:T(8,128)(2,1)} %bitcast.3, bf16[64,128,128]{2,1,0:T(8,128)(2,1)} %bitcast.2, f32[4,128,128]{2,1,0:T(8,128)} %wq_own.1, f32[128,128]{1,0:T(8,128)} %get-tuple-element.10.wq_got, f32[1,128,128]{2,1,0:T(8,128)} %wk_own.1, ...), custom_call_target="tpu_custom_call" | custom-call | tf_op jit(solution)/shard_map/compute/pallas_call | solution.py:316
  60.5 18.6 %reduce.1 = (f32[4,128,128]{2,1,0:T(8,128)}, f32[1,128,128]{2,1,0:T(8,128)}) custom-call(f32[128,128]{1,0:T(8,128)} %get-tuple-element.12.pq, f32[128,128]{1,0:T(8,128)} %get-tuple-element.13.pk), custom_call_target="tpu_custom_call" | custom-call | tf_op jit(solution)/shard_map/reduce/pallas_call | solution.py:491
  79.0 1.7 %copy.9 = f32[4,128,128]{2,1,0:T(8,128)} copy(f32[4,128,128]{2,1,0:T(8,128)} %get-tuple-element.16) | data formatting | bytes 524288
  80.7 1.5 %copy.10 = f32[1,128,128]{2,1,0:T(8,128)} copy(f32[1,128,128]{2,1,0:T(8,128)} %get-tuple-element.17) | data formatting | bytes 131072
